TPU v7x, 32 devices: a whole 2x2x4 slice. The times are simulated.
32 devices in a mesh: seq: 8 (over z, x), mem: 4 (over y, core).
Axes of the slice: x: 2, y: 2, z: 4, core: 2. Of those that a mesh axis runs over, the one named last changes fastest.
Arguments:
- queries: bfloat16 [4096, 2048], P(('seq', 'mem')), may hold values from -6 to 6
- keys: bfloat16 [4096, 2048], P(('seq', 'mem')), may hold values from -0.52734375 to 0.52734375
- values: bfloat16 [4096, 2048], P(('seq', 'mem')), may hold values from -6 to 6
- gamma: bfloat16 [4096, 16], P(('seq', 'mem')), as said below
- rate: bfloat16 [4, 16], replicated, as said below
- route_ids: int32 [4096, 2], P(('seq', 'mem')), may hold values from 0 to 3, all different within a row; in each aligned block of 128 rows (0 to 127, 128 to 255, ...) at most 96 rows name the same one
- route_weights: float32 [4096, 2], P(('seq', 'mem')), may hold values from 0.2 to 1
- norm_gain: float32 [2048], replicated, may hold values from 0.25 to 1.75
Outputs:
- mixed_out: bfloat16 [4096, 2048], P(('seq', 'mem'))
Inputs may be any that keep to these rules, and one draw needn't show every extreme that they name: `route_ids`: each token names two different memories. The tokens of one device name one memory at most 96 times; some memory is named exactly 96 times by some device's tokens. `gamma`: Positive; from 0.5 up to 6144. `rate`: Positive; from 0.04 * 4 / 4096 up to 0.06.
All inputs are finite; a program needn't handle non-finite values.
Results may differ from a plain program's by a relative error of at most 0.0052.
Values may be sent and summed in bfloat16 or wider, within the bound.
A program may use at most 128 MiB of HBM per device.

v0:
```python
import jax
import jax.numpy as jnp
from jax import lax
from jax.sharding import PartitionSpec as P

BLOCK = 128


epsilon = 1e-06


def carried_in(value, axis, join, neutral):
    count, mine = (lax.axis_size(axis), lax.axis_index(axis))
    pieces = jax.tree.map(lambda part: lax.all_gather(part, axis), value)
    total = jax.tree.map(
        lambda part, zero: jnp.full_like(part, 0) + jnp.asarray(zero, part.dtype), value, neutral
    )

    def turn(position, total):
        longer = join(total, jax.tree.map(lambda part: part[position], pieces))
        return jax.tree.map(lambda new, old: jnp.where(position < mine, new, old), longer, total)

    return lax.fori_loop(0, count - 1, turn, total)


def combine_state(earlier, later_part):
    return (earlier[0] * later_part[0], later_part[0][:, None, None] * earlier[1] + later_part[1])


def owner_heads(query_rows, key_rows, value_rows, gamma_rows, rate_rows):
    sources, capacity, head_count, head_width = query_rows.shape
    block_count = sources * capacity // BLOCK
    query_rows = query_rows.reshape(block_count, BLOCK, head_count, head_width)
    key_rows = key_rows.reshape(block_count, BLOCK, head_count, head_width)
    value_rows = value_rows.reshape(block_count, BLOCK, head_count, head_width)
    rate_now = rate_rows[0, 0].astype(jnp.float32)
    levels = jnp.cumsum(
        -rate_now[None, None, :]
        * gamma_rows.reshape(block_count, BLOCK, head_count).astype(jnp.float32),
        axis=1,
    )
    spread_log = levels[:, :, None, :] - levels[:, None, :, :]
    causal = (jnp.arange(BLOCK)[:, None] >= jnp.arange(BLOCK)[None, :])[None, :, :, None]
    decays = jnp.exp(jnp.where(causal, spread_log, -1e30))
    scores = jnp.einsum("bthd,bshd->btsh", query_rows, key_rows, preferred_element_type=jnp.float32)
    weights = (decays * scores).astype(jnp.bfloat16)
    intra_out = jnp.einsum(
        "btsh,bshe->bthe", weights, value_rows, preferred_element_type=jnp.float32
    )
    last_level = levels[:, -1, :]
    keyed_rows = (
        key_rows.astype(jnp.float32) * jnp.exp(last_level[:, None, :] - levels)[..., None]
    ).astype(jnp.bfloat16)
    updates = jnp.einsum(
        "bshd,bshe->bhde", keyed_rows, value_rows, preferred_element_type=jnp.float32
    )
    fading = jnp.exp(last_level)

    def local_step(carried, inputs_now):
        fade_now, update_now = inputs_now
        next_carry = (carried[0] * fade_now, fade_now[:, None, None] * carried[1] + update_now)
        return (next_carry, carried)

    start_fade = jnp.ones((head_count,), jnp.float32)
    start_state = jnp.zeros((head_count, head_width, head_width), jnp.float32)
    device_sum, entering = lax.scan(local_step, (start_fade, start_state), (fading, updates))
    before_fade, before_state = carried_in(
        device_sum, "seq", combine_state, (start_fade, start_state)
    )
    states = entering[1] + entering[0][:, :, None, None] * before_state[None]
    scaled_query = query_rows.astype(jnp.float32) * jnp.exp(levels)[..., None]
    inter_out = jnp.einsum("bthd,bhde->bthe", scaled_query, states, precision=lax.Precision.HIGHEST)
    raw_out = intra_out + inter_out
    normed = raw_out * lax.rsqrt(jnp.mean(raw_out * raw_out, axis=-1, keepdims=True) + epsilon)
    return normed.astype(jnp.bfloat16).reshape(sources, capacity, head_count, head_width)


def body(queries, keys, values, gamma, rate, route_ids, route_weights, norm_gain):
    token_count, feat_count = queries.shape
    head_count = gamma.shape[1]
    head_width = feat_count // head_count
    owners = lax.axis_size("mem")
    capacity = 3 * token_count // owners
    flat_routes = route_ids.reshape(-1)
    route_hits = (flat_routes[:, None] == jnp.arange(owners, dtype=jnp.int32)[None, :]).astype(
        jnp.int32
    )
    earlier_hits = jnp.cumsum(route_hits, axis=0) - route_hits
    route_rank = jnp.sum(route_hits * earlier_hits, axis=1)
    slot_ids = (flat_routes * capacity + route_rank).reshape(token_count, 2)
    slot_range = jnp.arange(owners * capacity, dtype=jnp.int32)
    chosen = (slot_ids[:, 0][None, :] == slot_range[:, None]) | (
        slot_ids[:, 1][None, :] == slot_range[:, None]
    )
    select = chosen.astype(jnp.bfloat16)

    def place_rows(row_block):
        return jnp.dot(select, row_block, preferred_element_type=jnp.float32).astype(jnp.bfloat16)

    send_query = place_rows(queries).reshape(owners, capacity, head_count, head_width)
    send_key = place_rows(keys).reshape(owners, capacity, head_count, head_width)
    send_value = place_rows(values).reshape(owners, capacity, head_count, head_width)
    send_gamma = place_rows(gamma).reshape(owners, capacity, head_count)
    send_rate = rate[:, None, :]
    arrived = (
        lax.all_to_all(send_query, "mem", split_axis=0, concat_axis=0, tiled=True),
        lax.all_to_all(send_key, "mem", split_axis=0, concat_axis=0, tiled=True),
        lax.all_to_all(send_value, "mem", split_axis=0, concat_axis=0, tiled=True),
        lax.all_to_all(send_gamma, "mem", split_axis=0, concat_axis=0, tiled=True),
        lax.all_to_all(send_rate, "mem", split_axis=0, concat_axis=0, tiled=True),
    )
    returned = lax.all_to_all(owner_heads(*arrived), "mem", split_axis=0, concat_axis=0, tiled=True)
    returned = returned.reshape(owners * capacity, feat_count)
    pick_first = (slot_ids[:, 0][:, None] == slot_range[None, :]).astype(jnp.bfloat16)
    pick_second = (slot_ids[:, 1][:, None] == slot_range[None, :]).astype(jnp.bfloat16)
    first_out = jnp.dot(pick_first, returned, preferred_element_type=jnp.float32)
    second_out = jnp.dot(pick_second, returned, preferred_element_type=jnp.float32)
    mixed_out = norm_gain[None, :] * (
        route_weights[:, 0:1] * first_out + route_weights[:, 1:2] * second_out
    )
    return mixed_out.astype(jnp.bfloat16)


def solution(mesh):
    in_specs = (
        P(("seq", "mem"), None),
        P(("seq", "mem"), None),
        P(("seq", "mem"), None),
        P(("seq", "mem"), None),
        P(),
        P(("seq", "mem"), None),
        P(("seq", "mem"), None),
        P(),
    )
    out_specs = P(("seq", "mem"), None)
    return jax.shard_map(body, mesh=mesh, in_specs=in_specs, out_specs=out_specs, check_vma=False)
```

profile of v0, /device:TPU:0, one launch (start us, length us, event | category | flops | bytes accessed | tf_op | source)
XLA Modules:
  0.0 279.7 jit_solution(11339378211645253428)
XLA Ops:
  7.9 4.3 %all-to-all-start.1 = ((bf16[4,1,16]{2,1,0:T(2,128)(2,1)}), bf16[4,1,16]{2,1,0:T(2,128)(2,1)S(1)}, u32[]{:S(2)}, u32[]{:S(2)}) async-start(bf16[4,1,16]{2,1,0:T(2,128)(2,1)} %copy.90), calls=%async_computation.1 | async-start | bytes 4096 | tf_op jit(solution)/shard_map/all_to_all | solution.py:110
  17.3 3.3 %all-to-all-start.2 = ((bf16[4,96,16]{1,2,0:T(8,128)(2,1)}), bf16[4,96,16]{1,2,0:T(8,128)(2,1)S(1)}, u32[]{:S(2)}, u32[]{:S(2)}) async-start(bf16[4,96,16]{1,2,0:T(8,128)(2,1)} %copy.91), calls=%async_computation.2 | async-start | bytes 32768 | tf_op jit(solution)/shard_map/all_to_all | solution.py:109
  21.2 1.6 copy.108
  22.8 1.7 all-to-all-done.2
  24.5 3.6 %all-to-all-start.3 = ((bf16[4,96,16,128]{3,2,1,0:T(8,128)(2,1)}), bf16[4,96,16,128]{3,2,1,0:T(8,128)(2,1)S(1)}, u32[]{:S(2)}, u32[]{:S(2)}) async-start(bf16[4,96,16,128]{3,2,1,0:T(8,128)(2,1)} %bitcast.112), calls=%async_computation.3 | async-start | bytes 3145728 | tf_op jit(solution)/shard_map/all_to_all | solution.py:107
  28.1 1.6 fusion.26
  29.7 1.6 copy.107
  31.3 16.8 %all-to-all-done.3 = bf16[4,96,16,128]{3,2,1,0:T(8,128)(2,1)S(1)} async-done(((bf16[4,96,16,128]{3,2,1,0:T(8,128)(2,1)}), bf16[4,96,16,128]{3,2,1,0:T(8,128)(2,1)S(1)}, u32[]{:S(2)}, u32[]{:S(2)}) %all-to-all-start.3) | async-done | bytes 1572896 | tf_op jit(solution)/shard_map/all_to_all | solution.py:107
  48.1 4.3 %all-to-all-start = ((bf16[4,96,16,128]{3,2,1,0:T(8,128)(2,1)}), bf16[4,96,16,128]{3,2,1,0:T(8,128)(2,1)}, u32[]{:S(2)}, u32[]{:S(2)}) async-start(bf16[4,96,16,128]{3,2,1,0:T(8,128)(2,1)} %bitcast.111), calls=%async_computation | async-start | bytes 3145728 | tf_op jit(solution)/shard_map/all_to_all | solution.py:108
  53.7 1.9 multiply_convert_fusion
  55.5 17.0 %all-to-all-done = bf16[4,96,16,128]{3,2,1,0:T(8,128)(2,1)} async-done(((bf16[4,96,16,128]{3,2,1,0:T(8,128)(2,1)}), bf16[4,96,16,128]{3,2,1,0:T(8,128)(2,1)}, u32[]{:S(2)}, u32[]{:S(2)}) %all-to-all-start) | async-done | bytes 1572896 | tf_op jit(solution)/shard_map/all_to_all | solution.py:108
  72.5 4.3 %fusion.16 = f32[3,16,128,128]{3,2,1,0:T(8,128)} fusion(bf16[3,128,16,128]{3,2,1,0:T(8,128)(2,1)} %multiply_convert_fusion, bf16[3,128,16,128]{3,2,1,0:T(8,128)(2,1)} %bitcast.5), kind=kOutput, calls=%fused_computation.33 | convolution fusion | flops 201326592 | bytes 6291456 | tf_op jit(solution)/shard_map/bshd,bshe->bhde/dot_general | solution.py:54
  76.8 13.5 %while.31 = (s32[]{:T(128)}, f32[16]{0:T(128)S(1)}, f32[16,128,128]{2,1,0:T(8,128)S(1)}, f32[3,16]{1,0:T(4,128)}, f32[3,16,128,128]{3,2,1,0:T(8,128)}, /*index=5...) while((s32[]{:T(128)}, f32[16]{0:T(128)S(1)}, ...), condition=%wide.region_5.6_spmd.clone, body=%wide.region_4.5_spmd.clone.sunk | while | flops 1048611 | bytes 5244021 | solution.py:66
  91.3 1.6 fusion.28
  92.9 1.6 copy.109
  94.6 4.5 %all-to-all-start.4 = ((bf16[4,96,16,128]{3,2,1,0:T(8,128)(2,1)}), bf16[4,96,16,128]{3,2,1,0:T(8,128)(2,1)}, u32[]{:S(2)}, u32[]{:S(2)}) async-start(bf16[4,96,16,128]{3,2,1,0:T(8,128)(2,1)} %bitcast.110), calls=%async_computation.4 | async-start | bytes 3145728 | tf_op jit(solution)/shard_map/all_to_all | solution.py:106
  101.9 23.4 %all-reduce = f32[128]{0:T(128)S(1)} all-reduce(f32[128]{0:T(128)S(1)} %dynamic-update-slice), channel_id=2, replica_groups=mesh['seq'=8,'mem'=4] {'seq'}, use_global_device_ids=true, to_apply=%add | all-reduce | flops 128 | bytes 1024
  125.4 3.3 %convert_multiply_fusion = f32[3,128,16,128]{3,2,1,0:T(8,128)} fusion(bf16[3,128,16,128]{3,2,1,0:T(8,128)(2,1)} %bitcast.9, f32[3,128,16]{2,1,0:T(8,128)S(1)} %get-tuple-element.214), kind=kLoop, calls=%fused_computation.18 | loop fusion | flops 1572864 | bytes 4743168 | tf_op jit(solution)/shard_map/mul | solution.py:71
  128.7 88.2 %all-gather.4.cloned.1.call-done = f32[128,128,128]{2,1,0:T(8,128)} async-done(((f32[16,128,128]{2,1,0:T(8,128)}), f32[128,128,128]{2,1,0:T(8,128)}) %all-gather.4.cloned.1.call-update) | async-done | bytes 8388624 | tf_op jit(solution)/shard_map/all_gather | solution.py:14
  216.9 10.4 %while.32 = (s32[]{:T(128)}, f32[16,128,128]{2,1,0:T(8,128)S(1)}, s32[]{:T(128)}, f32[8,16]{1,0:T(8,128)S(1)}, f32[8,16,128,128]{3,2,1,0:T(8,128)}, /*index=5*/s32[]{:T(128)}, s32[]{:T(128)}) while((s32[]{:T(128)}, f32[16,128,128]{2,1,0:T(8,128)S(1)}, s32[]{:T(128)}, f32[8,16]{1,0:T(8,128)S(1)}, f32[8,16,128,128]{3,2,1,0:T(8,128)}, ...), condition=%wide.region_7.8_spmd.clone, body=%wide.region_6.7_spmd.clone.sunk | while | flops 1048580 | bytes 3146025 | solution.py:23
  218.4 1.5 fusion.59
  219.9 1.5 fusion.59
  221.4 1.5 fusion.59
  222.9 1.5 fusion.59
  224.4 1.5 fusion.59
  225.9 1.5 fusion.59
  227.4 8.4 %fusion.7 = f32[3,16,128,128]{2,3,1,0:T(8,128)} fusion(f32[3,128,16,128]{3,2,1,0:T(8,128)} %convert_multiply_fusion, f32[3,16,128,128]{3,2,1,0:T(8,128)} %get-tuple-element.139, f32[16,128,128]{2,1,0:T(8,128)S(1)} %get-tuple-element.143, f32[3,16]{1,0:T(4,128)S(1)} %copy-done.9), kind=kOutput, calls=%fused_computation.16 | convolution fusion | flops 1209532416 | bytes 10485952 | tf_op jit(solution)/shard_map/bthd,bhde->bthe/dot_general | solution.py:72
  235.9 6.9 %fusion.4 = (f32[3,128,16]{1,2,0:T(8,128)S(1)}, f32[3,16,128,128]{2,3,1,0:T(8,128)}) fusion(f32[3,16,128,128]{2,3,1,0:T(8,128)} %fusion.7, bf16[3,128,16,128]{3,2,1,0:T(8,128)(2,1)} %bitcast.9, bf16[3,128,16,128]{3,2,1,0:T(8,128)(2,1)S(1)} %bitcast.109, f32[3,128,16]{1,2,0:T(8,128)S(1)} %copy-done.2, pred[128,128]{0,1:T(8,128)(4,1)S(1)} %iota_compare_fusion.6, ...), kind=kOutput, calls=%fused_computation.12 | convolution fusion | flops 408152064 | bytes 11075584 | tf_op jit(solution)/shard_map/btsh,bshe->bthe/dot_general | solution.py:47
  242.7 2.4 fusion.5
  245.1 2.2 copy.103
  247.3 3.7 %all-to-all-start.5 = ((bf16[4,96,16,128]{3,2,1,0:T(8,128)(2,1)}), bf16[4,96,16,128]{3,2,1,0:T(8,128)(2,1)S(1)}, u32[]{:S(2)}, u32[]{:S(2)}) async-start(bf16[4,96,16,128]{3,2,1,0:T(8,128)(2,1)} %bitcast.113), calls=%async_computation.5 | async-start | bytes 3145728 | tf_op jit(solution)/shard_map/all_to_all | solution.py:112
  251.1 20.0 %all-to-all-done.5 = bf16[4,96,16,128]{3,2,1,0:T(8,128)(2,1)S(1)} async-done(((bf16[4,96,16,128]{3,2,1,0:T(8,128)(2,1)}), bf16[4,96,16,128]{3,2,1,0:T(8,128)(2,1)S(1)}, u32[]{:S(2)}, u32[]{:S(2)}) %all-to-all-start.5) | async-done | bytes 1572896 | tf_op jit(solution)/shard_map/all_to_all | solution.py:112
  (94 shorter events, 28.3 us)
Async XLA Ops:
  6.5 14.1 %copy-start = (bf16[128,2048]{1,0:T(8,128)(2,1)S(1)}, bf16[128,2048]{1,0:T(8,128)(2,1)}, u32[]{:S(2)}) copy-start(bf16[128,2048]{1,0:T(8,128)(2,1)} %param.13) | copy-start | bytes 1572868
  7.9 9.5 %all-to-all-start.1 = ((bf16[4,1,16]{2,1,0:T(2,128)(2,1)}), bf16[4,1,16]{2,1,0:T(2,128)(2,1)S(1)}, u32[]{:S(2)}, u32[]{:S(2)}) async-start(bf16[4,1,16]{2,1,0:T(2,128)(2,1)} %copy.90), calls=%async_computation.1 | async-start | bytes 4096 | tf_op jit(solution)/shard_map/all_to_all | solution.py:110
  15.8 75.5 %copy-start.4 = (s32[128]{0:T(128)}, s32[128]{0:T(128)S(1)}, u32[]{:S(2)}) copy-start(s32[128]{0:T(128)S(1)} %get-tuple-element.218) | copy-start | bytes 1540
  15.8 75.5 %copy-start.6 = (s32[128]{0:T(128)}, s32[128]{0:T(128)S(1)}, u32[]{:S(2)}) copy-start(s32[128]{0:T(128)S(1)} %get-tuple-element.217) | copy-start | bytes 1540
  17.3 7.2 %all-to-all-start.2 = ((bf16[4,96,16]{1,2,0:T(8,128)(2,1)}), bf16[4,96,16]{1,2,0:T(8,128)(2,1)S(1)}, u32[]{:S(2)}, u32[]{:S(2)}) async-start(bf16[4,96,16]{1,2,0:T(8,128)(2,1)} %copy.91), calls=%async_computation.2 | async-start | bytes 32768 | tf_op jit(solution)/shard_map/all_to_all | solution.py:109
  24.5 23.6 %all-to-all-start.3 = ((bf16[4,96,16,128]{3,2,1,0:T(8,128)(2,1)}), bf16[4,96,16,128]{3,2,1,0:T(8,128)(2,1)S(1)}, u32[]{:S(2)}, u32[]{:S(2)}) async-start(bf16[4,96,16,128]{3,2,1,0:T(8,128)(2,1)} %bitcast.112), calls=%async_computation.3 | async-start | bytes 3145728 | tf_op jit(solution)/shard_map/all_to_all | solution.py:107
  48.1 24.5 %all-to-all-start = ((bf16[4,96,16,128]{3,2,1,0:T(8,128)(2,1)}), bf16[4,96,16,128]{3,2,1,0:T(8,128)(2,1)}, u32[]{:S(2)}, u32[]{:S(2)}) async-start(bf16[4,96,16,128]{3,2,1,0:T(8,128)(2,1)} %bitcast.111), calls=%async_computation | async-start | bytes 3145728 | tf_op jit(solution)/shard_map/all_to_all | solution.py:108
  52.4 164.5 %all-gather.4.cloned.1.call-start = ((), (), s32[]{:S(2)}) async-start(), calls=%async_computation.6 | async-start | bytes 9437184 | tf_op jit(solution)/shard_map/all_gather | solution.py:14
  90.3 1.0 copy-start.1
  90.3 2.6 copy-start.3
  94.6 4.5 %copy-start.11 = (u32[32]{0:T(128)S(1)}, u32[32]{0:T(128)}, u32[]{:S(2)}) copy-start(u32[32]{0:T(128)} %constant.68) | copy-start | bytes 388
  94.6 30.8 %all-to-all-start.4 = ((bf16[4,96,16,128]{3,2,1,0:T(8,128)(2,1)}), bf16[4,96,16,128]{3,2,1,0:T(8,128)(2,1)}, u32[]{:S(2)}, u32[]{:S(2)}) async-start(bf16[4,96,16,128]{3,2,1,0:T(8,128)(2,1)} %bitcast.110), calls=%async_computation.4 | async-start | bytes 3145728 | tf_op jit(solution)/shard_map/all_to_all | solution.py:106
  216.9 10.5 %copy-start.9 = (f32[3,16]{1,0:T(4,128)S(1)}, f32[3,16]{1,0:T(4,128)}, u32[]{:S(2)}) copy-start(f32[3,16]{1,0:T(4,128)} %get-tuple-element.140) | copy-start | bytes 580
  227.4 8.5 %copy-start.2 = (f32[3,128,16]{1,2,0:T(8,128)S(1)}, f32[3,128,16]{1,2,0:T(8,128)}, u32[]{:S(2)}) copy-start(f32[3,128,16]{1,2,0:T(8,128)} %copy.94) | copy-start | bytes 73732
  247.3 3.7 %copy-start.10 = (f32[128,2]{0,1:T(2,128)S(1)}, f32[128,2]{0,1:T(2,128)}, u32[]{:S(2)}) copy-start(f32[128,2]{0,1:T(2,128)} %param.18) | copy-start | bytes 3076
  247.3 23.7 %copy-start.7 = (s32[128]{0:T(128)S(1)}, s32[128]{0:T(128)}, u32[]{:S(2)}) copy-start(s32[128]{0:T(128)} %copy-done.6) | copy-start | bytes 1540
  247.3 23.7 %all-to-all-start.5 = ((bf16[4,96,16,128]{3,2,1,0:T(8,128)(2,1)}), bf16[4,96,16,128]{3,2,1,0:T(8,128)(2,1)S(1)}, u32[]{:S(2)}, u32[]{:S(2)}) async-start(bf16[4,96,16,128]{3,2,1,0:T(8,128)(2,1)} %bitcast.113), calls=%async_computation.5 | async-start | bytes 3145728 | tf_op jit(solution)/shard_map/all_to_all | solution.py:112
  251.1 20.5 %copy-start.5 = (s32[128]{0:T(128)S(1)}, s32[128]{0:T(128)}, u32[]{:S(2)}) copy-start(s32[128]{0:T(128)} %copy-done.4) | copy-start | bytes 1540
  251.1 20.5 %copy-start.8 = (f32[2048]{0:T(1024)S(1)}, f32[2048]{0:T(1024)}, u32[]{:S(2)}) copy-start(f32[2048]{0:T(1024)} %param.19) | copy-start | bytes 24580
Sparse Core Ops, SparseCore 0:
  91.4 125.4 all-gather.3
where the time goes:
time: 281 us; the launch traced here: 280 us
  waiting for transfers between devices  144 us (51%)
  other arithmetic  29.8 us (11%)
  matrix products  26 us (9%)
  starting transfers between devices  23.7 us (8%)
  blocking collectives  23.4 us (8%)
  local copies, waits for them, and re-layouts  18.5 us (7%)
  between operations  14.4 us (5%)
    all_gather x1, waiting for transfers between devices, carried_in(): pieces = jax.tree.map(lambda part: lax.all_gather(part, axis), value)  88.2 us
    unnamed x1, blocking collectives  23.4 us
    all_to_all x1, waiting for transfers between devices, body(): lax.all_to_all(owner_heads(*arrived), 'mem', split_axis=0, concat_axis=0,...  20 us
    all_to_all x1, waiting for transfers between devices, body(): lax.all_to_all(send_value, 'mem', split_axis=0, concat_axis=0, tiled=True)  17 us
    all_to_all x1, waiting for transfers between devices, body(): lax.all_to_all(send_key, 'mem', split_axis=0, concat_axis=0, tiled=True)  16.8 us
    select_n x7, other arithmetic, turn(): jnp.where(position < mine, new, old)  10.2 us
    dot_general x1, matrix products, owner_heads(): jnp.einsum('bthd,bhde->bthe', scaled_query, states, precision=lax.Precisi...  8.44 us
    unnamed x32, local copies, waits for them, and re-layouts  8.01 us
  transfers between devices with their start and end apart: 7, of which 5 were waited for; matrix products, arithmetic and copies ran while one was open for 8% of the time, Pallas kernels for 0%

commit v1 on v0

v1 whole, which is shorter than its diff:
```python
import functools

import jax
import jax.numpy as jnp
from jax import lax
from jax.experimental import pallas as pl
from jax.experimental.pallas import tpu as pltpu
from jax.sharding import PartitionSpec as P

EPSILON = 1e-06
FAR = 1e30
F32 = jnp.float32
BF16 = jnp.bfloat16


def dot(a, b, dims=((1,), (0,))):
    return lax.dot_general(a, b, (dims, ((), ())), preferred_element_type=F32)


def kernel(n, seqs, hl, mems, pair, q_ref, k_ref, v_ref, aux_ref, rate_ref, gain_ref, out_ref,
           qbuf, kbuf, vbuf, auxb, lrm, kew, adec, atot, apart, cols, pbuf, u32, ubf, upart,
           esend, erecv, sgrp, raw, outb,
           aux_s, aux_r, tok_s, tok_r, a_s, a_r, u_s, u_r, e_s, e_r, o_s, o_r):
    me = lax.axis_index("mem")
    pos = lax.axis_index("seq")
    tok = q_ref.shape[0]
    hd = qbuf.shape[-1]
    inner = lax.rem(pos, pair)
    even = inner == 0
    mate = pos + 1 - 2 * inner
    first = pos < pair
    last = pos + pair >= seqs
    rank = lax.div(pos, pair)

    def peer(step):
        return lax.rem(me + step, n)

    def lanes(head):
        return pl.ds(pl.multiple_of(head * hd, hd), hd)

    def token_copy(t, h, dst, slot):
        src, buf = ((k_ref, kbuf), (v_ref, vbuf), (q_ref, qbuf))[t]
        return pltpu.make_async_remote_copy(
            src_ref=src.at[:, lanes(dst * hl + h)], dst_ref=buf.at[slot, h],
            send_sem=tok_s.at[t, h, dst], recv_sem=tok_r.at[t, h, slot],
            device_id={"mem": dst}, device_id_type=pl.DeviceIdType.MESH)

    def aux_copy(dst, slot):
        return pltpu.make_async_remote_copy(
            src_ref=aux_ref, dst_ref=auxb.at[slot], send_sem=aux_s.at[dst], recv_sem=aux_r.at[slot],
            device_id={"mem": dst}, device_id_type=pl.DeviceIdType.MESH)

    def a_copy():
        return pltpu.make_async_remote_copy(
            src_ref=atot, dst_ref=apart, send_sem=a_s, recv_sem=a_r,
            device_id={"seq": mate}, device_id_type=pl.DeviceIdType.MESH)

    def u_copy(h):
        return pltpu.make_async_remote_copy(
            src_ref=ubf.at[h], dst_ref=upart.at[h], send_sem=u_s.at[h], recv_sem=u_r.at[h],
            device_id={"seq": mate}, device_id_type=pl.DeviceIdType.MESH)

    def e_copy(h):
        return pltpu.make_async_remote_copy(
            src_ref=esend.at[h], dst_ref=erecv.at[h], send_sem=e_s.at[h], recv_sem=e_r.at[h],
            device_id={"seq": lax.rem(pos + pair, seqs)}, device_id_type=pl.DeviceIdType.MESH)

    def out_copy(h, dst, slot):
        return pltpu.make_async_remote_copy(
            src_ref=outb.at[h, dst], dst_ref=out_ref.at[:, lanes(slot * hl + h)],
            send_sem=o_s.at[h, dst], recv_sem=o_r.at[h, slot],
            device_id={"mem": dst}, device_id_type=pl.DeviceIdType.MESH)

    barrier = pltpu.get_barrier_semaphore()

    def greet(**where):
        pl.semaphore_signal(barrier, inc=1, device_id=where, device_id_type=pl.DeviceIdType.MESH)

    for step in range(1, n):
        greet(mem=peer(step))
    greet(seq=mate)

    @pl.when(jnp.logical_not(first))
    def _():
        greet(seq=pos - pair)

    @pl.when(jnp.logical_not(last))
    def _():
        greet(seq=pos + pair)

    pl.semaphore_wait(barrier, n + jnp.minimum(rank, 1) + jnp.minimum(seqs // pair - 1 - rank, 1))

    for step in range(1, n):
        aux_copy(peer(step), me).start()
    for h in range(hl):
        for t in (0, 1):
            for step in range(1, n):
                token_copy(t, h, peer(step), me).start()
    for h in range(hl):
        for step in range(1, n):
            token_copy(2, h, peer(step), me).start()

    auxb[me] = aux_ref[...]
    for h in range(hl):
        kbuf[me, h] = k_ref[:, lanes(me * hl + h)]
        vbuf[me, h] = v_ref[:, lanes(me * hl + h)]
        qbuf[me, h] = q_ref[:, lanes(me * hl + h)]

    row_at = lax.broadcasted_iota(jnp.int32, (tok, tok), 0)
    col_at = lax.broadcasted_iota(jnp.int32, (tok, tok), 1)
    upper = (row_at <= col_at).astype(BF16)
    heads = hl * n
    for step in range(1, n):
        aux_copy(peer(step), peer(step)).wait_recv()

    rates = rate_ref[pl.ds(pl.multiple_of(me * hl * mems, hl * mems), hl * mems), :]
    total = jnp.zeros((hl * mems, tok), F32)
    mem_at = lax.broadcasted_iota(jnp.int32, (mems, tok), 0).astype(F32)
    for j in range(n):
        ids = [auxb[j, heads + r:heads + r + 1, :] for r in (0, 1)]
        wts = [auxb[j, heads + 2 + r:heads + 3 + r, :] for r in (0, 1)]
        hit = [ids[r] == mem_at for r in (0, 1)]
        mask = jnp.logical_or(hit[0], hit[1])
        gam = [auxb[j, pl.ds(me * hl + h, 1), :] for h in range(hl)]
        picked = jnp.concatenate([jnp.where(mask, g, 0.0) for g in gam], axis=0)
        level = -rates * dot(picked.astype(BF16), upper)
        here = jnp.concatenate([jnp.where(mask, 1.0, 0.0)] * hl, axis=0) > 0.5
        end = jnp.broadcast_to(level[:, tok - 1:tok], level.shape)
        lrm[j] = jnp.where(here, level, FAR)
        kew[j] = jnp.where(here, jnp.exp(end - level), 0.0)
        adec[j] = jnp.exp(end)
        for h in range(hl):
            own = level[h * mems:(h + 1) * mems]
            ahead = own + total[h * mems:(h + 1) * mems]
            rows = [jnp.sum(jnp.where(hit[r], own, 0.0), axis=0, keepdims=True) for r in (0, 1)]
            rows += [jnp.sum(jnp.where(hit[r], ahead, 0.0), axis=0, keepdims=True) for r in (0, 1)]
            cols[j, h] = jnp.concatenate(rows + ids + wts, axis=0).T
        total = total + end
    atot[...] = jnp.exp(total)
    a_copy().start()

    def update(h):
        for j in range(n):
            @pl.when(me != j)
            def _():
                token_copy(0, h, j, j).wait_recv()
                token_copy(1, h, j, j).wait_recv()
        state = jnp.zeros((mems * hd, hd), F32)
        for j in range(n):
            turned = kbuf[j, h].astype(F32).T
            keyed = jnp.concatenate(
                [(turned * kew[j, pl.ds(h * mems + m, 1), :]).astype(BF16) for m in range(mems)], axis=0)
            fresh = dot(keyed, vbuf[j, h])
            if j > 0:
                pbuf[h, j] = state.astype(BF16)
                state = jnp.concatenate(
                    [adec[j, pl.ds(h * mems + m, 1), :] * state[m * hd:(m + 1) * hd] for m in range(mems)],
                    axis=0) + fresh
            else:
                state = fresh
        u32[h] = state
        ubf[h] = state.astype(BF16)
        u_copy(h).start()

    def select(ident, parts):
        got = parts[0]
        for m in range(1, mems):
            got = jnp.where(ident == float(m), parts[m], got)
        return got

    def intra(h):
        for j in range(n):
            @pl.when(me != j)
            def _():
                token_copy(2, h, j, j).wait_recv()
        causal = row_at >= col_at
        for j in range(n):
            query, value = qbuf[j, h], vbuf[j, h]
            score = dot(query, kbuf[j, h], ((1,), (1,)))
            col = cols[j, h]
            rows = [lrm[j, pl.ds(h * mems + m, 1), :] for m in range(mems)]
            weights = []
            for r in (0, 1):
                spread = col[:, r:r + 1] - select(col[:, 4 + r:5 + r], rows)
                decay = jnp.exp(jnp.where(causal, spread, -FAR))
                weights.append((decay * score).astype(BF16))
            inside = dot(jnp.concatenate(weights, axis=0), value)
            if j > 0:
                before = [dot(query, pbuf[h, j, m * hd:(m + 1) * hd, :]) for m in range(mems)]
            for r in (0, 1):
                part = inside[r * tok:(r + 1) * tok]
                if j > 0:
                    part = part + jnp.exp(col[:, r:r + 1]) * select(col[:, 4 + r:5 + r], before)
                raw[h, j, r] = part

    def relay(h, carry):
        @pl.when(h == 0)
        def _():
            a_copy().wait_recv()

        u_copy(h).wait_recv()

        @pl.when(first)
        def _():
            erecv[h] = jnp.zeros(erecv.shape[1:], BF16)

        @pl.when(jnp.logical_not(first))
        def _():
            e_copy(h).wait_recv()

        @pl.when(jnp.logical_not(last))
        def _():
            for m in range(mems):
                at = slice(m * hd, (m + 1) * hd)
                mine, other = atot[pl.ds(h * mems + m, 1), :], apart[pl.ds(h * mems + m, 1), :]
                own = jnp.where(even, other, 1.0) * u32[h, at, :]
                both = own + jnp.where(even, 1.0, mine) * upart[h, at, :].astype(F32)
                esend[h, at, :] = (both + mine * other * erecv[h, at, :].astype(F32)).astype(BF16)
            e_copy(h).start()

        @pl.when(even)
        def _():
            sgrp[h] = erecv[h]

        @pl.when(jnp.logical_not(even))
        def _():
            for m in range(mems):
                at = slice(m * hd, (m + 1) * hd)
                other = apart[pl.ds(h * mems + m, 1), :]
                sgrp[h, at, :] = (other * erecv[h, at, :].astype(F32) + upart[h, at, :].astype(F32)).astype(BF16)

        return carry

    def due(phase):
        return jnp.clip(phase - 1 - 2 * rank, 0, hl)

    def phase_step(phase, carry):
        @pl.when(phase < hl)
        def _():
            update(phase)

        @pl.when(phase >= hl)
        def _():
            intra(phase - hl)

        lax.fori_loop(due(phase), due(phase + 1), relay, 0)
        return carry

    lax.fori_loop(0, 2 * hl, phase_step, 0)
    relayed = due(2 * hl)

    def finish(h, carry):
        @pl.when(h >= relayed)
        def _():
            relay(h, 0)

        gain = gain_ref[pl.ds(me * hl + h, 1), :]
        for j in range(n):
            query, col = qbuf[j, h], cols[j, h]
            before = [dot(query, sgrp[h, m * hd:(m + 1) * hd, :]) for m in range(mems)]
            mixed = jnp.zeros((tok, hd), F32)
            for r in (0, 1):
                part = raw[h, j, r] + jnp.exp(col[:, 2 + r:3 + r]) * select(col[:, 4 + r:5 + r], before)
                scale = lax.rsqrt(jnp.mean(part * part, axis=-1, keepdims=True) + EPSILON)
                mixed = mixed + col[:, 6 + r:7 + r] * (part * scale).astype(BF16).astype(F32)
            done = (mixed * gain).astype(BF16)

            @pl.when(me == j)
            def _():
                out_ref[:, lanes(me * hl + h)] = done

            @pl.when(me != j)
            def _():
                outb[h, j] = done
                out_copy(h, j, me).start()
        return carry

    lax.fori_loop(0, hl, finish, 0)

    for step in range(1, n):
        there = peer(step)
        aux_copy(there, me).wait_send()
        for h in range(hl):
            for t in range(3):
                token_copy(t, h, there, me).wait_send()
            out_copy(h, there, me).wait_send()
            out_copy(h, there, there).wait_recv()
    a_copy().wait_send()
    for h in range(hl):
        u_copy(h).wait_send()

        @pl.when(jnp.logical_not(last))
        def _():
            e_copy(h).wait_send()


def body(n, seqs, queries, keys, values, gamma, rate, route_ids, route_weights, norm_gain):
    tok, feats = queries.shape
    heads = gamma.shape[1]
    mems = rate.shape[0]
    hd = feats // heads
    hl = heads // n
    pair = 2
    aux = jnp.concatenate([gamma.astype(F32), route_ids.astype(F32), route_weights], axis=1).T
    aux = jnp.pad(aux, ((0, -aux.shape[0] % 8), (0, 0)))
    rates = jnp.broadcast_to(rate.astype(F32).T.reshape(heads * mems, 1), (heads * mems, tok))
    gain = norm_gain.reshape(heads, hd)
    vm = pltpu.VMEM
    dma = pltpu.SemaphoreType.DMA
    rows = hl * mems
    scratch = [
        vm((n, hl, tok, hd), BF16), vm((n, hl, tok, hd), BF16), vm((n, hl, tok, hd), BF16),
        vm((n,) + aux.shape, F32),
        vm((n, rows, tok), F32), vm((n, rows, tok), F32), vm((n, rows, tok), F32),
        vm((rows, tok), F32), vm((rows, tok), F32),
        vm((n, hl, tok, 8), F32),
        vm((hl, n, mems * hd, hd), BF16),
        vm((hl, mems * hd, hd), F32), vm((hl, mems * hd, hd), BF16), vm((hl, mems * hd, hd), BF16),
        vm((hl, mems * hd, hd), BF16), vm((hl, mems * hd, hd), BF16), vm((hl, mems * hd, hd), BF16),
        vm((hl, n, 2, tok, hd), F32),
        vm((hl, n, tok, hd), BF16),
        dma((n,)), dma((n,)), dma((3, hl, n)), dma((3, hl, n)), dma, dma,
        dma((hl,)), dma((hl,)), dma((hl,)), dma((hl,)), dma((hl, n)), dma((hl, n)),
    ]
    spec = pl.BlockSpec(memory_space=pltpu.VMEM)
    return pl.pallas_call(
        functools.partial(kernel, n, seqs, hl, mems, pair),
        out_shape=jax.ShapeDtypeStruct((tok, feats), BF16),
        in_specs=[spec] * 6,
        out_specs=spec,
        scratch_shapes=scratch,
        compiler_params=pltpu.CompilerParams(
            collective_id=0, has_side_effects=True, vmem_limit_bytes=60 * 1024 * 1024),
    )(queries, keys, values, aux, rates, gain)


def solution(mesh):
    rows = P(("seq", "mem"), None)
    in_specs = (rows, rows, rows, rows, P(), rows, rows, P())
    run = functools.partial(body, mesh.shape["mem"], mesh.shape["seq"])
    return jax.shard_map(run, mesh=mesh, in_specs=in_specs, out_specs=rows, check_vma=False)
```

time: 281 us -> 49.9 us (0.18)
  the two profiles are of different devices: /device:TPU:0 before, /device:TPU:31 now
where the time goes in v1:
time: 49.9 us; the launch traced here: 49.6 us
  Pallas kernels  43.6 us (87%)
  local copies, waits for them, and re-layouts  5.97 us (12%)
    pallas_call x1, Pallas kernels, body(): pl.pallas_call(functools.partial(kernel, n, seqs, hl, mems, pair), out_sh...  43.6 us
    unnamed x9, local copies, waits for them, and re-layouts  4.51 us

profile of v1, /device:TPU:31, one launch (start us, length us, event | category | flops | bytes accessed | tf_op | source)
XLA Modules:
  0.0 49.6 jit_solution(17174741360032108955)
XLA Ops:
  0.0 0.0 copy-start.3
  0.0 0.7 %copy-done.3 = s32[128,2]{0,1:T(2,128)S(1)} copy-done((s32[128,2]{0,1:T(2,128)S(1)}, s32[128,2]{0,1:T(2,128)}, u32[]{:S(2)}) %copy-start.3) | copy-done | bytes 1048
  0.7 0.0 copy-start.1
  0.7 0.7 %copy-done.1 = bf16[4,16]{1,0:T(4,128)(2,1)S(1)} copy-done((bf16[4,16]{1,0:T(4,128)(2,1)S(1)}, bf16[4,16]{1,0:T(4,128)(2,1)}, u32[]{:S(2)}) %copy-start.1) | copy-done | bytes 152
  1.4 0.1 copy.10
  1.4 0.0 copy-start
  1.5 0.1 reshape.6
  1.5 0.6 %copy-done = bf16[128,16]{0,1:T(8,128)(2,1)S(1)} copy-done((bf16[128,16]{0,1:T(8,128)(2,1)S(1)}, bf16[128,16]{0,1:T(8,128)(2,1)}, u32[]{:S(2)}) %copy-start) | copy-done | bytes 4120
  2.1 0.0 copy-start.2
  2.1 0.7 %copy-done.2 = f32[128,2]{0,1:T(2,128)S(1)} copy-done((f32[128,2]{0,1:T(2,128)S(1)}, f32[128,2]{0,1:T(2,128)}, u32[]{:S(2)}) %copy-start.2) | copy-done | bytes 1048
  2.8 0.6 %pad.4.aux_ref = f32[24,128]{1,0:T(8,128)} pad(f32[20,128]{1,0:T(8,128)S(1)} %maximum_bitcast_fusion, f32[]{:T(128)} %constant.2.clone.1), padding=0_4x0_0 | pad | bytes 22532 | tf_op jit(solution)/shard_map/jit(_pad)/pad | solution.py:305
  3.4 0.7 %broadcast_in_dim.12.rate_ref = f32[64,128]{1,0:T(8,128)} broadcast(f32[64]{0:T(128)S(1)} %reshape.6), dimensions={0} | broadcast | bytes 33024 | tf_op jit(solution)/shard_map/broadcast_in_dim | solution.py:306
  4.1 43.6 %shard_map.82 = bf16[128,2048]{1,0:T(8,128)(2,1)} custom-call(bf16[128,2048]{1,0:T(8,128)(2,1)} %q_ref.1, bf16[128,2048]{1,0:T(8,128)(2,1)} %k_ref.1, bf16[128,2048]{1,0:T(8,128)(2,1)} %v_ref.1, f32[24,128]{1,0:T(8,128)} %pad.4.aux_ref, f32[64,128]{1,0:T(8,128)} %broadcast_in_dim.12.rate_ref, f32[16,128]{1,0:T(8,128)} %bitcast.5), custom_call_target="tpu_custom_call" | custom-call | tf_op jit(solution)/shard_map/pallas_call | solution.py:326
  47.8 1.9 %copy.12 = bf16[128,2048]{1,0:T(8,128)(2,1)} copy(bf16[128,2048]{1,0:T(8,128)(2,1)} %shard_map.82) | data formatting | bytes 1048576
  (4 shorter events, 0.0 us)
Async XLA Ops:
  0.0 0.7 %copy-start.3 = (s32[128,2]{0,1:T(2,128)S(1)}, s32[128,2]{0,1:T(2,128)}, u32[]{:S(2)}) copy-start(s32[128,2]{0,1:T(2,128)} %param.13) | copy-start | bytes 3076
  0.7 0.7 %copy-start.1 = (bf16[4,16]{1,0:T(4,128)(2,1)S(1)}, bf16[4,16]{1,0:T(4,128)(2,1)}, u32[]{:S(2)}) copy-start(bf16[4,16]{1,0:T(4,128)(2,1)} %param.12) | copy-start | bytes 388
  1.4 0.7 %copy-start = (bf16[128,16]{0,1:T(8,128)(2,1)S(1)}, bf16[128,16]{0,1:T(8,128)(2,1)}, u32[]{:S(2)}) copy-start(bf16[128,16]{0,1:T(8,128)(2,1)} %param.11) | copy-start | bytes 12292
  2.1 0.7 %copy-start.2 = (f32[128,2]{0,1:T(2,128)S(1)}, f32[128,2]{0,1:T(2,128)}, u32[]{:S(2)}) copy-start(f32[128,2]{0,1:T(2,128)} %param.14) | copy-start | bytes 3076

commit v2 on v1

--- a/solution.py
+++ b/solution.py
@@ -17,7 +17,8 @@
     return lax.dot_general(a, b, (dims, ((), ())), preferred_element_type=F32)
 
 
-def kernel(n, seqs, hl, mems, pair, q_ref, k_ref, v_ref, aux_ref, rate_ref, gain_ref, out_ref,
+def kernel(n, seqs, hl, mems, pair, q_ref, k_ref, v_ref, gamma_ref, rate_ref,
+           ids_ref, wts_ref, gain_ref, out_ref, aux_ref,
            qbuf, kbuf, vbuf, auxb, lrm, kew, adec, atot, apart, cols, pbuf, u32, ubf, upart,
            esend, erecv, sgrp, raw, outb,
            aux_s, aux_r, tok_s, tok_r, a_s, a_r, u_s, u_r, e_s, e_r, o_s, o_r):
@@ -55,14 +56,14 @@
             src_ref=atot, dst_ref=apart, send_sem=a_s, recv_sem=a_r,
             device_id={"seq": mate}, device_id_type=pl.DeviceIdType.MESH)
 
-    def u_copy(h):
-        return pltpu.make_async_remote_copy(
-            src_ref=ubf.at[h], dst_ref=upart.at[h], send_sem=u_s.at[h], recv_sem=u_r.at[h],
+    def u_copy(h, m):
+        return pltpu.make_async_remote_copy(
+            src_ref=ubf.at[h, m], dst_ref=upart.at[h, m], send_sem=u_s.at[h, m], recv_sem=u_r.at[h, m],
             device_id={"seq": mate}, device_id_type=pl.DeviceIdType.MESH)
 
-    def e_copy(h):
-        return pltpu.make_async_remote_copy(
-            src_ref=esend.at[h], dst_ref=erecv.at[h], send_sem=e_s.at[h], recv_sem=e_r.at[h],
+    def e_copy(h, m):
+        return pltpu.make_async_remote_copy(
+            src_ref=esend.at[h, m], dst_ref=erecv.at[h, m], send_sem=e_s.at[h, m], recv_sem=e_r.at[h, m],
             device_id={"seq": lax.rem(pos + pair, seqs)}, device_id_type=pl.DeviceIdType.MESH)
 
     def out_copy(h, dst, slot):
@@ -87,6 +88,17 @@
     @pl.when(jnp.logical_not(last))
     def _():
         greet(seq=pos + pair)
+
+    row_at = lax.broadcasted_iota(jnp.int32, (tok, tok), 0)
+    col_at = lax.broadcasted_iota(jnp.int32, (tok, tok), 1)
+    heads = hl * n
+    eye = (row_at == col_at).astype(BF16)
+    aux_ref[0:heads, :] = dot(gamma_ref[...], eye, ((0,), (0,)))
+    aux_ref[heads:heads + 2, :] = dot(ids_ref[...].astype(BF16), eye, ((0,), (0,)))
+    aux_ref[heads + 2:heads + 4, :] = lax.dot_general(
+        wts_ref[...], eye.astype(F32), (((0,), (0,)), ((), ())),
+        precision=lax.Precision.HIGHEST, preferred_element_type=F32)
+    aux_ref[heads + 4:, :] = jnp.zeros((aux_ref.shape[0] - heads - 4, tok), F32)
 
     pl.semaphore_wait(barrier, n + jnp.minimum(rank, 1) + jnp.minimum(seqs // pair - 1 - rank, 1))
 
@@ -106,14 +118,14 @@
         vbuf[me, h] = v_ref[:, lanes(me * hl + h)]
         qbuf[me, h] = q_ref[:, lanes(me * hl + h)]
 
-    row_at = lax.broadcasted_iota(jnp.int32, (tok, tok), 0)
-    col_at = lax.broadcasted_iota(jnp.int32, (tok, tok), 1)
     upper = (row_at <= col_at).astype(BF16)
-    heads = hl * n
     for step in range(1, n):
         aux_copy(peer(step), peer(step)).wait_recv()
 
-    rates = rate_ref[pl.ds(pl.multiple_of(me * hl * mems, hl * mems), hl * mems), :]
+    table = rate_ref[...].astype(F32)
+    head_at = lax.broadcasted_iota(jnp.int32, table.shape, 1)
+    rates = jnp.concatenate(
+        [jnp.sum(jnp.where(head_at == me * hl + h, table, 0.0), axis=1, keepdims=True) for h in range(hl)], axis=0)
     total = jnp.zeros((hl * mems, tok), F32)
     mem_at = lax.broadcasted_iota(jnp.int32, (mems, tok), 0).astype(F32)
     for j in range(n):
@@ -158,9 +170,10 @@
                     axis=0) + fresh
             else:
                 state = fresh
-        u32[h] = state
-        ubf[h] = state.astype(BF16)
-        u_copy(h).start()
+        for m in range(mems):
+            u32[h, m] = state[m * hd:(m + 1) * hd]
+            ubf[h, m] = state[m * hd:(m + 1) * hd].astype(BF16)
+            u_copy(h, m).start()
 
     def select(ident, parts):
         got = parts[0]
@@ -198,66 +211,43 @@
         def _():
             a_copy().wait_recv()
 
-        u_copy(h).wait_recv()
-
-        @pl.when(first)
-        def _():
-            erecv[h] = jnp.zeros(erecv.shape[1:], BF16)
-
-        @pl.when(jnp.logical_not(first))
-        def _():
-            e_copy(h).wait_recv()
-
-        @pl.when(jnp.logical_not(last))
-        def _():
-            for m in range(mems):
-                at = slice(m * hd, (m + 1) * hd)
-                mine, other = atot[pl.ds(h * mems + m, 1), :], apart[pl.ds(h * mems + m, 1), :]
-                own = jnp.where(even, other, 1.0) * u32[h, at, :]
-                both = own + jnp.where(even, 1.0, mine) * upart[h, at, :].astype(F32)
-                esend[h, at, :] = (both + mine * other * erecv[h, at, :].astype(F32)).astype(BF16)
-            e_copy(h).start()
-
-        @pl.when(even)
-        def _():
-            sgrp[h] = erecv[h]
-
-        @pl.when(jnp.logical_not(even))
-        def _():
-            for m in range(mems):
-                at = slice(m * hd, (m + 1) * hd)
-                other = apart[pl.ds(h * mems + m, 1), :]
-                sgrp[h, at, :] = (other * erecv[h, at, :].astype(F32) + upart[h, at, :].astype(F32)).astype(BF16)
-
+        def one(m, inside):
+            mine, other = atot[pl.ds(h * mems + m, 1), :], apart[pl.ds(h * mems + m, 1), :]
+            u_copy(h, m).wait_recv()
+
+            @pl.when(first)
+            def _():
+                erecv[h, m] = jnp.zeros((hd, hd), BF16)
+
+            @pl.when(jnp.logical_not(first))
+            def _():
+                e_copy(h, m).wait_recv()
+
+            @pl.when(jnp.logical_not(last))
+            def _():
+                both = jnp.where(even, other, 1.0) * u32[h, m]
+                both = both + jnp.where(even, 1.0, mine) * upart[h, m].astype(F32)
+                esend[h, m] = (both + mine * other * erecv[h, m].astype(F32)).astype(BF16)
+                e_copy(h, m).start()
+
+            @pl.when(even)
+            def _():
+                sgrp[h, m] = erecv[h, m]
+
+            @pl.when(jnp.logical_not(even))
+            def _():
+                sgrp[h, m] = (other * erecv[h, m].astype(F32) + upart[h, m].astype(F32)).astype(BF16)
+
+            return inside
+
+        lax.fori_loop(0, mems, one, 0)
         return carry
 
-    def due(phase):
-        return jnp.clip(phase - 1 - 2 * rank, 0, hl)
-
-    def phase_step(phase, carry):
-        @pl.when(phase < hl)
-        def _():
-            update(phase)
-
-        @pl.when(phase >= hl)
-        def _():
-            intra(phase - hl)
-
-        lax.fori_loop(due(phase), due(phase + 1), relay, 0)
-        return carry
-
-    lax.fori_loop(0, 2 * hl, phase_step, 0)
-    relayed = due(2 * hl)
-
-    def finish(h, carry):
-        @pl.when(h >= relayed)
-        def _():
-            relay(h, 0)
-
-        gain = gain_ref[pl.ds(me * hl + h, 1), :]
+    def finish(h):
+        gain = gain_ref[:, lanes(me * hl + h)]
         for j in range(n):
             query, col = qbuf[j, h], cols[j, h]
-            before = [dot(query, sgrp[h, m * hd:(m + 1) * hd, :]) for m in range(mems)]
+            before = [dot(query, sgrp[h, m]) for m in range(mems)]
             mixed = jnp.zeros((tok, hd), F32)
             for r in (0, 1):
                 part = raw[h, j, r] + jnp.exp(col[:, 2 + r:3 + r]) * select(col[:, 4 + r:5 + r], before)
@@ -273,9 +263,27 @@
             def _():
                 outb[h, j] = done
                 out_copy(h, j, me).start()
+
+    def due(phase):
+        return jnp.clip(jnp.maximum(phase - 1 - 2 * rank, phase - 2 * hl + 1), 0, hl)
+
+    def phase_step(phase, carry):
+        @pl.when(phase < hl)
+        def _():
+            update(phase)
+
+        @pl.when(jnp.logical_and(phase >= hl, phase < 2 * hl))
+        def _():
+            intra(phase - hl)
+
+        @pl.when(phase >= 2 * hl)
+        def _():
+            finish(phase - 2 * hl)
+
+        lax.fori_loop(due(phase), due(phase + 1), relay, 0)
         return carry
 
-    lax.fori_loop(0, hl, finish, 0)
+    lax.fori_loop(0, 3 * hl, phase_step, 0)
 
     for step in range(1, n):
         there = peer(step)
@@ -287,11 +295,12 @@
             out_copy(h, there, there).wait_recv()
     a_copy().wait_send()
     for h in range(hl):
-        u_copy(h).wait_send()
-
-        @pl.when(jnp.logical_not(last))
-        def _():
-            e_copy(h).wait_send()
+        for m in range(mems):
+            u_copy(h, m).wait_send()
+
+            @pl.when(jnp.logical_not(last))
+            def _():
+                e_copy(h, m).wait_send()
 
 
 def body(n, seqs, queries, keys, values, gamma, rate, route_ids, route_weights, norm_gain):
@@ -301,37 +310,35 @@
     hd = feats // heads
     hl = heads // n
     pair = 2
-    aux = jnp.concatenate([gamma.astype(F32), route_ids.astype(F32), route_weights], axis=1).T
-    aux = jnp.pad(aux, ((0, -aux.shape[0] % 8), (0, 0)))
-    rates = jnp.broadcast_to(rate.astype(F32).T.reshape(heads * mems, 1), (heads * mems, tok))
-    gain = norm_gain.reshape(heads, hd)
+    aux_rows = -(-(heads + 4) // 8) * 8
     vm = pltpu.VMEM
     dma = pltpu.SemaphoreType.DMA
     rows = hl * mems
     scratch = [
+        vm((aux_rows, tok), F32),
         vm((n, hl, tok, hd), BF16), vm((n, hl, tok, hd), BF16), vm((n, hl, tok, hd), BF16),
-        vm((n,) + aux.shape, F32),
+        vm((n, aux_rows, tok), F32),
         vm((n, rows, tok), F32), vm((n, rows, tok), F32), vm((n, rows, tok), F32),
         vm((rows, tok), F32), vm((rows, tok), F32),
         vm((n, hl, tok, 8), F32),
         vm((hl, n, mems * hd, hd), BF16),
-        vm((hl, mems * hd, hd), F32), vm((hl, mems * hd, hd), BF16), vm((hl, mems * hd, hd), BF16),
-        vm((hl, mems * hd, hd), BF16), vm((hl, mems * hd, hd), BF16), vm((hl, mems * hd, hd), BF16),
+        vm((hl, mems, hd, hd), F32), vm((hl, mems, hd, hd), BF16), vm((hl, mems, hd, hd), BF16),
+        vm((hl, mems, hd, hd), BF16), vm((hl, mems, hd, hd), BF16), vm((hl, mems, hd, hd), BF16),
         vm((hl, n, 2, tok, hd), F32),
         vm((hl, n, tok, hd), BF16),
         dma((n,)), dma((n,)), dma((3, hl, n)), dma((3, hl, n)), dma, dma,
-        dma((hl,)), dma((hl,)), dma((hl,)), dma((hl,)), dma((hl, n)), dma((hl, n)),
+        dma((hl, mems)), dma((hl, mems)), dma((hl, mems)), dma((hl, mems)), dma((hl, n)), dma((hl, n)),
     ]
     spec = pl.BlockSpec(memory_space=pltpu.VMEM)
     return pl.pallas_call(
         functools.partial(kernel, n, seqs, hl, mems, pair),
         out_shape=jax.ShapeDtypeStruct((tok, feats), BF16),
-        in_specs=[spec] * 6,
+        in_specs=[spec] * 8,
         out_specs=spec,
         scratch_shapes=scratch,
         compiler_params=pltpu.CompilerParams(
             collective_id=0, has_side_effects=True, vmem_limit_bytes=60 * 1024 * 1024),
-    )(queries, keys, values, aux, rates, gain)
+    )(queries, keys, values, gamma, rate, route_ids, route_weights, norm_gain.reshape(1, feats))
 
 
 def solution(mesh):

time: 49.9 us -> 46.1 us (0.924)
  Pallas kernels: 43.6 us -> 40.9 us
  local copies, waits for them, and re-layouts: 5.97 us -> 4.77 us
    pallas_call x1, Pallas kernels: 43.6 us -> 40.9 us  [body(): pl.pallas_call(functools.partial(kernel, n, seqs, hl, mems, pair), out_sh...]
    broadcast_in_dim x3 -> x0, local copies, waits for them, and re-layouts: 0.86 us -> none  [body(): jnp.broadcast_to(rate.astype(F32).T.reshape(heads * mems, 1), (heads * me...]
    pad x1 -> x0, local copies, waits for them, and re-layouts: 0.6 us -> none  [body(): aux = jnp.pad(aux, ((0, -aux.shape[0] % 8), (0, 0)))]
    unnamed x9 -> x8, local copies, waits for them, and re-layouts: 4.51 us -> 4.77 us
where the time goes in v2:
time: 46.1 us; the launch traced here: 45.7 us
  Pallas kernels  40.9 us (89%)
  local copies, waits for them, and re-layouts  4.77 us (10%)
    pallas_call x1, Pallas kernels, body(): pl.pallas_call(functools.partial(kernel, n, seqs, hl, mems, pair), out_sh...  40.9 us
    unnamed x8, local copies, waits for them, and re-layouts  4.77 us

profile of v2, /device:TPU:31, one launch (start us, length us, event | category | flops | bytes accessed | tf_op | source)
XLA Modules:
  0.0 45.7 jit_solution(14041012522894758250)
XLA Ops:
  0.0 0.0 copy-start
  0.0 1.4 %copy.9.gamma_ref = bf16[128,16]{1,0:T(8,128)(2,1)} copy(bf16[128,16]{0,1:T(8,128)(2,1)} %param.11) | data formatting | bytes 8192 | tf_op args[3]
  1.4 0.0 copy-done
  1.4 0.0 copy-start.1
  1.4 0.7 %copy.10.ids_ref = s32[128,2]{1,0:T(8,128)} copy(s32[128,2]{0,1:T(2,128)S(1)} %copy-done) | data formatting | bytes 2048 | tf_op args[5]
  2.2 0.0 copy-done.1
  2.2 0.7 %copy.11.wts_ref = f32[128,2]{1,0:T(8,128)} copy(f32[128,2]{0,1:T(2,128)S(1)} %copy-done.1) | data formatting | bytes 2048 | tf_op args[6]
  2.9 40.9 %shard_map.82 = bf16[128,2048]{1,0:T(8,128)(2,1)} custom-call(bf16[128,2048]{1,0:T(8,128)(2,1)} %q_ref.1, bf16[128,2048]{1,0:T(8,128)(2,1)} %k_ref.1, bf16[128,2048]{1,0:T(8,128)(2,1)} %v_ref.1, bf16[128,16]{1,0:T(8,128)(2,1)} %copy.9.gamma_ref, bf16[4,16]{1,0:T(4,128)(2,1)} %rate_ref.1, s32[128,2]{1,0:T(8,128)} %copy.10.ids_ref, f32[128,2]{1,0:T(8,128)} %copy.11.wts_ref, ...), custom_call_target="tpu_custom_call" | custom-call | tf_op jit(solution)/shard_map/pallas_call | solution.py:333
  43.8 1.9 %copy.13 = bf16[128,2048]{1,0:T(8,128)(2,1)} copy(bf16[128,2048]{1,0:T(8,128)(2,1)} %shard_map.82) | data formatting | bytes 1048576
Async XLA Ops:
  0.0 1.4 %copy-start = (s32[128,2]{0,1:T(2,128)S(1)}, s32[128,2]{0,1:T(2,128)}, u32[]{:S(2)}) copy-start(s32[128,2]{0,1:T(2,128)} %param.13) | copy-start | bytes 3076
  1.4 0.7 %copy-start.1 = (f32[128,2]{0,1:T(2,128)S(1)}, f32[128,2]{0,1:T(2,128)}, u32[]{:S(2)}) copy-start(f32[128,2]{0,1:T(2,128)} %param.14) | copy-start | bytes 3076
